TPU v7x, 32 devices: a whole 2x2x4 slice. The times are simulated.
32 devices in a mesh: rep: 2 (over y), pipe: 2 (over core), tp: 8 (over z, x).
Axes of the slice: x: 2, y: 2, z: 4, core: 2. Of those that a mesh axis runs over, the one named last changes fastest.
Arguments:
- hidden_entering: bfloat16 [2, 120, 8192], P('rep', None, 'tp'), parts along dimension 0, may hold values from -60 to 60
- segment_adapter: int32 [2, 3], P('rep'), parts along dimension 0, may hold values from 0 to 127, as said below
- segment_requests: int32 [2, 3], P('rep'), parts along dimension 0, may hold values from 10 to 40, as said below
- section_norm_gain: float32 [2, 8192], P('pipe'), may hold values from 0.25 to 1.75
- up_matrix: bfloat16 [2, 14336, 8192], P('pipe', 'tp'), may hold values from -0.0625 to 0.0625
- down_matrix: bfloat16 [2, 8192, 14336], P('pipe', 'tp'), may hold values from -0.046875 to 0.046875
- adapter_reduce: bfloat16 [2, 128, 131072], P('pipe', None, 'tp'), may hold values from -0.0625 to 0.0625
- adapter_expand: bfloat16 [2, 128, 229376], P('pipe', None, 'tp'), may hold values from -1.5 to 1.5
Outputs:
- section_out: bfloat16 [2, 2, 120, 8192], P('pipe', 'rep', None, 'tp'), parts along dimension 1
There are 2 independent parts, one for each index of `rep`. A program takes and returns all parts, laid end to end along the dimension named above; an argument that names none is the same for every part. Nothing has to cross between parts.
Inputs may be any that keep to these rules, and one draw needn't show every extreme that they name: `segment_adapter`: within each micro-batch the adapter ids of its segments do not decrease. The first segment_requests[m, j] rows of segment j of micro-batch m hold requests; the other rows are padding.
All inputs are finite; a program needn't handle non-finite values.
Results may differ from a plain program's by a relative error of at most 0.0045.
Values may be sent and summed in bfloat16 or wider, within the bound.
A program may use at most 128 MiB of HBM per device.

v0:
```python
import jax
import jax.numpy as jnp
from jax import lax
from jax.sharding import PartitionSpec as P

EPSILON = 1e-05


def shifted(x, axis, by):
    size = lax.axis_size(axis)
    pairs = [(i, i + by) for i in range(size) if 0 <= i + by < size]
    return lax.ppermute(x, axis, pairs)


def times_rows(left, weight):
    return lax.dot_general(
        left, weight, (((1,), (1,)), ((), ())), preferred_element_type=jnp.float32
    )


def block_step(
    current, unit_ids, unit_live, gain_full, up_weight, down_weight, shrink_weight, expand_weight
):
    row_count = current.shape[0]
    col_count = current.shape[1]
    hid_count = up_weight.shape[0]
    segments = unit_ids.shape[0]
    seg_rows = row_count // segments
    feature_width = gain_full.shape[0]
    adapter_rank_count = shrink_weight.shape[1] // col_count
    column = lax.axis_index("tp") * col_count
    gain_mine = lax.dynamic_slice_in_dim(gain_full, column, col_count, 0)
    widened_local = current.astype(jnp.float32)
    local_scaled = (widened_local * gain_mine).astype(jnp.bfloat16)
    input_panel = shrink_weight[unit_ids].reshape(segments, col_count, adapter_rank_count)
    output_panel = expand_weight[unit_ids].reshape(segments, hid_count, adapter_rank_count)
    partial_value = jnp.einsum(
        "sdr,spd->rsp",
        input_panel,
        local_scaled.reshape(segments, seg_rows, col_count),
        preferred_element_type=jnp.float32,
    ).reshape(adapter_rank_count, row_count)
    local_squares = jnp.sum(widened_local * widened_local, axis=1)
    reduced, squares = lax.psum((partial_value, local_squares), "tp")
    widened = lax.all_gather(current, "tp", axis=1, tiled=True).astype(jnp.float32)
    scaled = (widened * gain_full).astype(jnp.bfloat16)
    up_total = times_rows(scaled, up_weight)
    inverse = lax.rsqrt(squares / feature_width + EPSILON)
    low_rank = (
        (reduced * inverse[None, :])
        .astype(jnp.bfloat16)
        .reshape(adapter_rank_count, segments, seg_rows)
    )
    adapted = jnp.einsum(
        "rsp,sdr->spd", low_rank, output_panel, preferred_element_type=jnp.float32
    ).reshape(row_count, hid_count)
    up_sum = inverse[:, None] * up_total + adapted
    hidden_act = jax.nn.silu(up_sum).astype(jnp.bfloat16)
    down_sum = times_rows(lax.all_gather(hidden_act, "tp", axis=1, tiled=True), down_weight)
    updated = (widened_local + down_sum).astype(jnp.bfloat16)
    positions = lax.broadcasted_iota(jnp.int32, (segments, seg_rows), 1)
    row_kept = (positions < unit_live[:, None]).reshape(row_count, 1)
    return jnp.where(row_kept, updated, jnp.zeros_like(updated))


def run_window(
    units, unit_ids, unit_live, gain_full, up_weight, down_weight, shrink_weight, expand_weight
):
    section_index = lax.axis_index("pipe")
    sections = lax.axis_size("pipe")
    unit_count = units.shape[0]
    tick_total = unit_count + sections - 1

    def process(tick_index, received, collected):
        position = jnp.clip(tick_index - section_index, 0, unit_count - 1)
        arriving = lax.dynamic_index_in_dim(
            units, jnp.minimum(tick_index, unit_count - 1), 0, keepdims=False
        )
        current = jnp.where(section_index == 0, arriving, received)
        ids_here = lax.dynamic_index_in_dim(unit_ids, position, 0, keepdims=False)
        live_here = lax.dynamic_index_in_dim(unit_live, position, 0, keepdims=False)
        produced = block_step(
            current,
            ids_here,
            live_here,
            gain_full,
            up_weight,
            down_weight,
            shrink_weight,
            expand_weight,
        )
        lag = tick_index - section_index
        in_window = jnp.logical_and(lag >= 0, lag < unit_count)
        placed = lax.dynamic_update_index_in_dim(collected, produced, position, 0)
        return (produced, jnp.where(in_window, placed, collected))

    def one_tick(tick_index, state):
        produced, collected = process(tick_index, state[0], state[1])
        return (shifted(produced, "pipe", 1), collected)

    start_state = (jnp.zeros_like(units[0]), jnp.zeros_like(units))
    received, collected = lax.fori_loop(0, tick_total - 1, one_tick, start_state)
    produced, collected = process(tick_total - 1, received, collected)
    return collected


def per_device(
    hidden_entering,
    segment_adapter,
    segment_requests,
    section_norm_gain,
    up_matrix,
    down_matrix,
    adapter_reduce,
    adapter_expand,
):
    batch_list = hidden_entering.shape[0]
    row_count = hidden_entering.shape[1]
    col_count = hidden_entering.shape[2]
    collected = run_window(
        hidden_entering,
        segment_adapter,
        segment_requests,
        section_norm_gain[0],
        up_matrix[0],
        down_matrix[0],
        adapter_reduce[0],
        adapter_expand[0],
    )
    return collected.reshape(1, batch_list, row_count, col_count)


def solution(mesh):
    return jax.shard_map(
        per_device,
        mesh=mesh,
        in_specs=(
            P("rep", None, "tp"),
            P("rep", None),
            P("rep", None),
            P("pipe", None),
            P("pipe", "tp", None),
            P("pipe", "tp", None),
            P("pipe", None, "tp"),
            P("pipe", None, "tp"),
        ),
        out_specs=P("pipe", "rep", None, "tp"),
        check_vma=False,
    )
```

profile of v0, /device:TPU:1, one launch (start us, length us, event | category | flops | bytes accessed | tf_op | source)
XLA Modules:
  0.0 301.2 jit_solution(11378490578715964258)
XLA Ops:
  6.5 1.8 fusion.50
  8.4 0.7 fusion.60
  9.1 3.5 %gather_fusion = bf16[3,16384]{1,0:T(4,128)(2,1)S(1)} fusion(bf16[128,16384]{1,0:T(8,128)(2,1)} %bitcast.75, s32[1024]{0:T(1024)S(1)} %pad_clamp_fusion), kind=kCustom, calls=%fused_computation | custom fusion | bytes 196620 | tf_op jit(solution)/shard_map/while/body/eval_jaxpr/gather | solution.py:35
  12.6 0.6 reshape.115
  13.2 0.7 constant_dynamic-slice_fusion
  13.9 0.3 convolution_bitcast_fusion.1
  14.3 0.1 reshape.116
  14.4 19.7 %all-reduce.1 = (f32[16,120]{1,0:T(8,128)S(1)}, f32[120]{0:T(128)S(1)}) all-reduce(f32[16,120]{1,0:T(8,128)S(1)} %reshape.116, f32[120]{0:T(128)S(1)} %get-tuple-element.37), channel_id=1, replica_groups=mesh['rep'=2,'pipe'=2,'tp'=8] {'tp'}, use_global_device_ids=true, to_apply=%region_2.3 | all-reduce | flops 2040 | bytes 16320 | tf_op jit(solution)/shard_map/while/body/eval_jaxpr/psum | solution.py:44
  34.1 0.1 reshape.117
  34.2 4.9 %gather_fusion.1 = bf16[3,28672]{1,0:T(4,128)(2,1)S(1)} fusion(bf16[128,28672]{1,0:T(8,128)(2,1)} %bitcast.74, s32[1024]{0:T(1024)S(1)} %pad_clamp_fusion), kind=kCustom, calls=%fused_computation.1 | custom fusion | bytes 344076 | tf_op jit(solution)/shard_map/while/body/eval_jaxpr/gather | solution.py:36
  39.1 1.0 reshape.118
  40.2 0.6 fusion.58
  40.8 17.3 %all-gather.5.cloned.1.call-done = bf16[120,8192]{1,0:T(8,128)(2,1)} async-done(((bf16[120,1024]{1,0:T(8,128)(2,1)}), bf16[120,8192]{1,0:T(8,128)(2,1)}) %all-gather.5.cloned.1.call-update) | async-done | bytes 1966096 | tf_op jit(solution)/shard_map/while/body/eval_jaxpr/all_gather | solution.py:45
  58.1 15.4 %multiply_convert_fusion.7 = bf16[120,1792]{1,0:T(8,128)(2,1)} fusion(f32[120,1792]{1,0:T(8,128)S(1)} %bitcast.73, bf16[1,1792,8192]{2,1,0:T(8,128)(2,1)} %param.12, bf16[120,8192]{1,0:T(8,128)(2,1)} %all-gather.5.cloned.1.call-done, f32[8192]{0:T(1024)S(1)} %bitcast.78, f32[120]{0:T(128)S(1)} %add_rsqrt_fusion.1), kind=kOutput, calls=%fused_computation.29 | convolution fusion | flops 3527669760 | bytes 32649696 | tf_op jit(solution)/shard_map/while/body/eval_jaxpr/dot_general | solution.py:16
  73.6 0.1 iota_compare_fusion
  73.7 0.1 lt.71
  73.7 62.2 %all-gather.7.cloned.1.call-done = bf16[120,14336]{1,0:T(8,128)(2,1)} async-done(((bf16[120,1792]{1,0:T(8,128)(2,1)}), bf16[120,14336]{1,0:T(8,128)(2,1)}) %all-gather.7.cloned.1.call-update) | async-done | bytes 3440656 | tf_op jit(solution)/shard_map/while/body/eval_jaxpr/all_gather | solution.py:59
  135.9 14.8 %fusion.34 = bf16[120,1024]{1,0:T(8,128)(2,1)S(1)} fusion(bf16[120,14336]{1,0:T(8,128)(2,1)} %all-gather.7.cloned.1.call-done, bf16[1,1024,14336]{2,1,0:T(8,128)(2,1)} %param.13, bf16[120,1024]{1,0:T(8,128)(2,1)S(1)} %copy-done.1, pred[120]{0:T(512)(128)(4,1)S(1)} %lt.71), kind=kOutput, calls=%fused_computation.24 | convolution fusion | flops 3523706880 | bytes 33292408 | tf_op jit(solution)/shard_map/while/body/eval_jaxpr/dot_general | solution.py:16
  150.7 1.3 collective-permute-start
  152.0 3.4 %collective-permute-done = bf16[120,1024]{1,0:T(8,128)(2,1)S(1)} collective-permute-done((bf16[120,1024]{1,0:T(8,128)(2,1)S(1)}, bf16[120,1024]{1,0:T(8,128)(2,1)S(1)}, u32[]{:S(2)}, u32[]{:S(2)}) %collective-permute-start) | collective-permute-done | bytes 245792 | tf_op jit(solution)/shard_map/while/body/eval_jaxpr/ppermute | solution.py:12
  155.4 0.9 fusion.51
  156.3 0.0 all-gather.11.cloned.1.call-start
  156.3 1.0 fusion.52
  157.3 0.4 convolution_bitcast_fusion
  157.7 0.1 reshape.121
  157.8 16.7 %all-reduce = (f32[16,120]{1,0:T(8,128)S(1)}, f32[120]{0:T(128)S(1)}) all-reduce(f32[16,120]{1,0:T(8,128)S(1)} %reshape.121, f32[120]{0:T(128)S(1)} %get-tuple-element.35), channel_id=1, replica_groups=mesh['rep'=2,'pipe'=2,'tp'=8] {'tp'}, use_global_device_ids=true, to_apply=%region_5.6 | all-reduce | flops 2040 | bytes 16320 | tf_op jit(solution)/shard_map/psum | solution.py:44
  174.6 0.1 reshape.122
  174.7 0.6 fusion.56
  175.3 26.1 %all-gather.9.cloned.1.call-done = bf16[120,8192]{1,0:T(8,128)(2,1)} async-done(((bf16[120,1024]{1,0:T(8,128)(2,1)}), bf16[120,8192]{1,0:T(8,128)(2,1)}) %all-gather.9.cloned.1.call-update) | async-done | bytes 1966096 | tf_op jit(solution)/shard_map/all_gather | solution.py:45
  201.3 15.4 %multiply_convert_fusion.4 = bf16[120,1792]{1,0:T(8,128)(2,1)} fusion(f32[120,1792]{1,0:T(8,128)S(1)} %bitcast.72, bf16[1,1792,8192]{2,1,0:T(8,128)(2,1)} %param.12, bf16[120,8192]{1,0:T(8,128)(2,1)} %all-gather.9.cloned.1.call-done, f32[8192]{0:T(1024)S(1)} %bitcast.79, f32[120]{0:T(128)S(1)} %add_rsqrt_fusion), kind=kOutput, calls=%fused_computation.28 | convolution fusion | flops 3527669760 | bytes 32649696 | tf_op jit(solution)/shard_map/dot_general | solution.py:16
  216.8 62.4 %all-gather.11.cloned.1.call-done = bf16[120,14336]{1,0:T(8,128)(2,1)} async-done(((bf16[120,1792]{1,0:T(8,128)(2,1)}), bf16[120,14336]{1,0:T(8,128)(2,1)}) %all-gather.11.cloned.1.call-update) | async-done | bytes 3440656 | tf_op jit(solution)/shard_map/all_gather | solution.py:59
  279.1 15.5 %fusion.43 = bf16[1,1,120,1024]{3,2,1,0:T(8,128)(2,1)} fusion(bf16[120,14336]{1,0:T(8,128)(2,1)} %all-gather.11.cloned.1.call-done, bf16[1,1024,14336]{2,1,0:T(8,128)(2,1)} %param.13, bf16[120,1024]{1,0:T(8,128)(2,1)S(1)} %copy-done, bf16[120,1024]{1,0:T(8,128)(2,1)S(1)} %fusion.34, pred[120]{0:T(512)(128)(4,1)S(1)} %lt.71, pred[]{:T(512)S(6)} %and.10, ...), kind=kOutput, calls=%fused_computation.27 | convolution fusion | flops 3523952640 | bytes 33538170 | tf_op jit(solution)/shard_map/dot_general | solution.py:16
  (25 shorter events, 0.3 us)
Async XLA Ops:
  6.5 51.5 %all-gather.5.cloned.1.call-start = ((), (), s32[]{:S(2)}) async-start(), calls=%async_computation | async-start | bytes 2211840 | tf_op jit(solution)/shard_map/while/body/eval_jaxpr/all_gather | solution.py:45
  8.4 127.5 %all-gather.7.cloned.1.call-start = ((), (), s32[]{:S(2)}) async-start(), calls=%async_computation.1 | async-start | bytes 3870720 | tf_op jit(solution)/shard_map/while/body/eval_jaxpr/all_gather | solution.py:59
  13.9 44.2 %copy-start.3 = (f32[1,8192]{1,0:T(1,128)S(1)}, f32[1,8192]{1,0:T(1,128)}, u32[]{:S(2)}) copy-start(f32[1,8192]{1,0:T(1,128)} %param.11) | copy-start | bytes 98308
  58.1 15.5 %copy-start.4 = (s32[1,3]{1,0:T(1,128)S(1)}, s32[1,3]{1,0:T(1,128)}, u32[]{:S(2)}) copy-start(s32[1,3]{1,0:T(1,128)} %param.10) | copy-start | bytes 40
  58.1 77.8 %copy-start.1 = (bf16[120,1024]{1,0:T(8,128)(2,1)S(1)}, bf16[120,1024]{1,0:T(8,128)(2,1)}, u32[]{:S(2)}) copy-start(bf16[120,1024]{1,0:T(8,128)(2,1)} %get-tuple-element.38) | copy-start | bytes 737284
  73.5 127.8 %all-gather.9.cloned.1.call-start = ((), (), s32[]{:S(2)}) async-start(), calls=%async_computation.2 | async-start | bytes 2211840 | tf_op jit(solution)/shard_map/all_gather | solution.py:45
  73.7 81.6 %copy-start.2 = (bf16[1,120,1024]{2,1,0:T(8,128)(2,1)S(1)}, bf16[1,120,1024]{2,1,0:T(8,128)(2,1)}, u32[]{:S(2)}) copy-start(bf16[1,120,1024]{2,1,0:T(8,128)(2,1)} %param.8) | copy-start | bytes 737284
  150.7 4.7 %collective-permute-start = (bf16[120,1024]{1,0:T(8,128)(2,1)S(1)}, bf16[120,1024]{1,0:T(8,128)(2,1)S(1)}, u32[]{:S(2)}, u32[]{:S(2)}) collective-permute-start(bf16[120,1024]{1,0:T(8,128)(2,1)S(1)} %fusion.34), channel_id=1, source_target_pairs={{0,8},{1,9},{2,10},{3,11},{4,12},{5,13},{6,14},{7,15},{16,24},{17,... | collective-permute-start | bytes 737288 | tf_op jit(solution)/shard_map/while/body/eval_jaxpr/ppermute | solution.py:12
  156.3 122.9 %all-gather.11.cloned.1.call-start = ((), (), s32[]{:S(2)}) async-start(), calls=%async_computation.3 | async-start | bytes 3870720 | tf_op jit(solution)/shard_map/all_gather | solution.py:59
  201.3 77.8 %copy-start = (bf16[120,1024]{1,0:T(8,128)(2,1)S(1)}, bf16[120,1024]{1,0:T(8,128)(2,1)}, u32[]{:S(2)}) copy-start(bf16[120,1024]{1,0:T(8,128)(2,1)} %get-tuple-element.36) | copy-start | bytes 737284
Sparse Core Ops, SparseCore 0:
  9.5 48.5 all-gather.4
  73.6 62.2 all-gather.6
  156.4 44.9 all-gather.8
  216.9 62.2 all-gather.10
where the time goes:
time: 304 us; the launch traced here: 301 us
  waiting for transfers between devices  171 us (56%)
  matrix products  63 us (21%)
  blocking collectives  36.5 us (12%)
  between operations  13.3 us (4%)
  local copies, waits for them, and re-layouts  11.2 us (4%)
  other arithmetic  4.47 us (1%)
    all_gather x2, waiting for transfers between devices, block_step(): lax.all_gather(hidden_act, 'tp', axis=1, tiled=True)  125 us
    dot_general x4, matrix products, times_rows(): lax.dot_general(left, weight, (((1,), (1,)), ((), ())), preferred_element...  61.1 us
    all_gather x2, waiting for transfers between devices, block_step(): lax.all_gather(current, 'tp', axis=1, tiled=True).astype(jnp.float32)  43.4 us
    psum x2, blocking collectives, block_step(): reduced, squares = lax.psum((partial_value, local_squares), 'tp')  36.5 us
  transfers between devices with their start and end apart: 5, of which 5 were waited for; matrix products, arithmetic and copies ran while one was open for 5% of the time, Pallas kernels for 0%

commit v1 on v0

--- a/solution.py
+++ b/solution.py
@@ -1,6 +1,10 @@
+import functools
+
 import jax
 import jax.numpy as jnp
 from jax import lax
+from jax.experimental import pallas as pl
+from jax.experimental.pallas import tpu as pltpu
 from jax.sharding import PartitionSpec as P
 
 EPSILON = 1e-05
@@ -63,6 +67,318 @@
     return jnp.where(row_kept, updated, jnp.zeros_like(updated))
 
 
+MESH = pl.DeviceIdType.MESH
+PIECE = 256
+COLUMNS = 2
+VMEM_BYTES = 67_043_328
+
+
+def section_kernel(
+    x_ref, gain_ref, keep_ref, reduce_ref, expand_ref, up_hbm, down_hbm, out_ref,
+    up_v, down_v, xs, act, current, acc, partial,
+    up_sem, down_sem, part_send, part_recv, x_send, x_recv, a_send, a_recv, pipe_sem,
+):
+    shards, x_pieces, rows, _ = xs.shape
+    a_pieces = act.shape[1]
+    cols = x_ref.shape[1]
+    hidden = up_v.shape[0]
+    width = shards * cols
+    segments = reduce_ref.shape[0]
+    rank = reduce_ref.shape[1]
+    seg_rows = rows // segments
+    depth = shards // COLUMNS
+    me = lax.axis_index("tp")
+    stage = lax.axis_index("pipe")
+    stages = lax.axis_size("pipe")
+    z, x = me // COLUMNS, me % COLUMNS
+    partner = z * COLUMNS + (1 - x)
+
+    def up_copy(c):
+        span = pl.ds(c * PIECE, PIECE)
+        return pltpu.make_async_copy(up_hbm.at[span, :], up_v.at[span, :], up_sem.at[c])
+
+    def down_copy(t):
+        span = pl.ds(pl.multiple_of(t * hidden, 128), hidden)
+        return pltpu.make_async_copy(down_hbm.at[:, span], down_v.at[:, span], down_sem.at[t])
+
+    @pl.loop(0, a_pieces)
+    def _(c):
+        up_copy(c).start()
+
+    @pl.loop(0, shards)
+    def _(i):
+        down_copy((me + i) % shards).start()
+
+    barrier = pltpu.get_barrier_semaphore()
+
+    @pl.loop(1, shards)
+    def _(i):
+        pl.semaphore_signal(barrier, inc=1, device_id={"tp": (me + i) % shards}, device_id_type=MESH)
+
+    @pl.when(stage > 0)
+    def _():
+        pl.semaphore_signal(barrier, inc=1, device_id={"pipe": stage - 1}, device_id_type=MESH)
+
+    @pl.when(stage < stages - 1)
+    def _():
+        pl.semaphore_signal(barrier, inc=1, device_id={"pipe": stage + 1}, device_id_type=MESH)
+
+    neighbours = jnp.where(stage > 0, 1, 0) + jnp.where(stage < stages - 1, 1, 0)
+    pl.semaphore_wait(barrier, shards - 1 + neighbours)
+
+    def hand_over():
+        return pltpu.make_async_remote_copy(
+            src_ref=out_ref, dst_ref=current, send_sem=pipe_sem.at[0], recv_sem=pipe_sem.at[1],
+            device_id={"pipe": (stage + 1) % stages}, device_id_type=MESH)
+
+    @pl.when(stage == 0)
+    def _():
+        current[...] = x_ref[...]
+
+    @pl.when(stage > 0)
+    def _():
+        hand_over().wait_recv()
+
+    class Spread:
+        def __init__(self, buf, send, recv, pieces):
+            self.buf, self.send, self.recv, self.pieces = buf, send, recv, pieces
+
+        def copy(self, t, c, way, target):
+            return pltpu.make_async_remote_copy(
+                src_ref=self.buf.at[t, c], dst_ref=self.buf.at[t, c],
+                send_sem=self.send.at[way, t, c], recv_sem=self.recv.at[t, c],
+                device_id={"tp": target}, device_id_type=MESH)
+
+        def each(self, source_z, c, do):
+            t = source_z * COLUMNS + x
+
+            @pl.when(jnp.logical_and(source_z <= z, z < depth - 1))
+            def _():
+                do(self.copy(t, c, 0, (me + COLUMNS) % shards))
+
+            @pl.when(jnp.logical_and(source_z >= z, z > 0))
+            def _():
+                do(self.copy(t, c, 1, (me + shards - COLUMNS) % shards))
+
+            do(self.copy(t, c, 2, partner))
+
+        def forward(self, source_z, c):
+            self.each(source_z, c, lambda d: d.start())
+
+        def arrive(self, t, c):
+            self.copy(t, c, 2, partner).wait_recv()
+
+        def relay(self, step, c):
+            @pl.when(z >= step)
+            def _():
+                self.arrive((z - step) * COLUMNS + x, c)
+                self.forward(z - step, c)
+
+            @pl.when(z + step < depth)
+            def _():
+                self.arrive((z + step) * COLUMNS + x, c)
+                self.forward(z + step, c)
+
+        def partner_arrive(self, t):
+            @pl.loop(0, self.pieces)
+            def _(c):
+                self.arrive(t, c)
+
+        def drain(self):
+            @pl.loop(0, depth)
+            def _(source_z):
+                @pl.loop(0, self.pieces)
+                def _(c):
+                    self.each(source_z, c, lambda d: d.wait_send())
+
+    x_side = Spread(xs, x_send, x_recv, x_pieces)
+    a_side = Spread(act, a_send, a_recv, a_pieces)
+
+    for c in range(x_pieces):
+        gain = gain_ref[:, pl.ds(pl.multiple_of(me * cols + c * PIECE, 128), PIECE)]
+        wide = current[:, c * PIECE:(c + 1) * PIECE].astype(jnp.float32)
+        xs[me, c] = (wide * gain).astype(jnp.bfloat16)
+        x_side.forward(z, c)
+
+    lane_seg = lax.broadcasted_iota(jnp.int32, (1, 128), 1) // seg_rows
+    nt = (((1,), (1,)), ((), ()))
+    total = jnp.zeros((segments * rank, 128), jnp.float32)
+    squares = jnp.zeros((8, 128), jnp.float32)
+    lane_pad = 128 - rows
+    for c in range(x_pieces):
+        span = slice(c * PIECE, (c + 1) * PIECE)
+        mine = jnp.concatenate([xs[me, c], jnp.zeros((lane_pad, PIECE), jnp.bfloat16)], axis=0) if lane_pad else xs[me, c]
+        panel = reduce_ref[:, :, span].reshape(segments * rank, PIECE)
+        total += lax.dot_general(panel, mine, nt, preferred_element_type=jnp.float32)
+        wide = current[:, span].astype(jnp.float32)
+        square = wide * wide
+        if lane_pad:
+            square = jnp.concatenate([square, jnp.zeros((lane_pad, PIECE), jnp.float32)], axis=0)
+        squares += lax.dot_general(jnp.ones((8, PIECE), jnp.float32), square, nt,
+                                   precision=lax.Precision.HIGHEST, preferred_element_type=jnp.float32)
+    picked = jnp.zeros((rank, 128), jnp.float32)
+    for s in range(segments):
+        picked += jnp.where(lane_seg == s, total[s * rank:(s + 1) * rank], 0.0)
+    partial[me, 0:rank] = picked
+    partial[me, rank:rank + 8] = squares
+
+    def part_copy(owner, target):
+        return pltpu.make_async_remote_copy(
+            src_ref=partial.at[owner], dst_ref=partial.at[owner], send_sem=part_send.at[target],
+            recv_sem=part_recv.at[owner], device_id={"tp": target}, device_id_type=MESH)
+
+    @pl.loop(1, shards)
+    def _(i):
+        part_copy(me, (me + i) % shards).start()
+
+    for step in range(1, depth):
+        @pl.loop(0, x_pieces)
+        def _(c):
+            x_side.relay(step, c)
+
+    @pl.loop(1, shards)
+    def _(i):
+        owner = (me + i) % shards
+        part_copy(owner, owner).wait_recv()
+
+    summed = partial[0]
+    for t in range(1, shards):
+        summed = summed + partial[t]
+    inverse_lane = lax.rsqrt(summed[rank:rank + 1] / width + EPSILON)
+    low_lane = (summed[0:rank] * inverse_lane).astype(jnp.bfloat16).astype(jnp.float32)
+    blocks = [jnp.where(lane_seg == s, low_lane, 0.0) for s in range(segments)]
+    blocks.append(jnp.broadcast_to(inverse_lane, (8, 128)))
+    blocks.append(jnp.zeros((128 - segments * rank - 8, 128), jnp.float32))
+    turned = jnp.transpose(jnp.concatenate(blocks, axis=0))[:rows]
+    low_rank = turned[:, :segments * rank].astype(jnp.bfloat16)
+    inverse = turned[:, segments * rank:segments * rank + 1]
+
+    @pl.loop(0, depth)
+    def _(source_z):
+        x_side.partner_arrive(source_z * COLUMNS + (1 - x))
+
+    LAG = 2
+
+    def relays(k):
+        for step in range(1, depth):
+            c = k - LAG * step
+
+            @pl.when(jnp.logical_and(c >= 0, c < a_pieces))
+            def _():
+                a_side.relay(step, c)
+
+    @pl.loop(0, a_pieces)
+    def _(k):
+        up_copy(k).wait()
+        span = pl.ds(pl.multiple_of(k * PIECE, PIECE), PIECE)
+        base = jnp.zeros((rows, PIECE), jnp.float32)
+        for t in range(shards):
+            for c in range(x_pieces):
+                at = t * cols + c * PIECE
+                base += lax.dot_general(xs[t, c], up_v[span, at:at + PIECE], nt, preferred_element_type=jnp.float32)
+        panel = expand_ref[:, :, span].reshape(segments * rank, PIECE)
+        adapted = jnp.dot(low_rank, panel, preferred_element_type=jnp.float32)
+        value = inverse * base + adapted
+        act[me, k] = (value / (1.0 + jnp.exp(-value))).astype(jnp.bfloat16)
+        a_side.forward(z, k)
+        relays(k)
+
+    acc[...] = current[...].astype(jnp.float32)
+
+    def down_part(t):
+        down_copy(t).wait()
+
+        @pl.loop(0, cols // PIECE)
+        def _(n):
+            block = pl.ds(pl.multiple_of(n * PIECE, PIECE), PIECE)
+            part = acc[:, block]
+            for c in range(a_pieces):
+                span = pl.ds(pl.multiple_of(t * hidden + c * PIECE, 128), PIECE)
+                part += lax.dot_general(act[t, c], down_v[block, span], nt, preferred_element_type=jnp.float32)
+            acc[:, block] = part
+
+    def down_at(z_of, column):
+        @pl.when(jnp.logical_and(z_of >= 0, z_of < depth))
+        def _():
+            t = z_of * COLUMNS + column
+
+            @pl.when(column != x)
+            def _():
+                a_side.partner_arrive(t)
+
+            down_part(t)
+
+    order = [(0, 0), (0, 1), (1, 0), (-1, 0), (2, 0), (-2, 0)]
+    rest = [(d * sign, o) for d in range(1, depth) for o in (0, 1) for sign in (1, -1)]
+    rest = [item for item in rest if item not in order]
+    ticks = LAG * (depth - 1)
+    for j in range(ticks):
+        relays(a_pieces + j)
+        if j < len(order):
+            far, other = order[j]
+            down_at(z + far, (x + other) % COLUMNS)
+    for far, other in order[ticks:] + rest:
+        down_at(z + far, (x + other) % COLUMNS)
+
+    out_ref[...] = jnp.where(keep_ref[...] > 0.0, acc[...], 0.0).astype(jnp.bfloat16)
+
+    @pl.when(stage < stages - 1)
+    def _():
+        copy = hand_over()
+        copy.start()
+        copy.wait_send()
+
+    @pl.loop(1, shards)
+    def _(i):
+        part_copy(me, (me + i) % shards).wait_send()
+
+    x_side.drain()
+    a_side.drain()
+
+
+def fused_sections(current, ids, live, gain, up_weight, down_weight, shrink_weight, expand_weight):
+    rows, cols = current.shape
+    hidden = up_weight.shape[0]
+    segments = ids.shape[0]
+    shards = lax.axis_size("tp")
+    rank = shrink_weight.shape[1] // cols
+
+    def panels(table, length):
+        picked = [lax.dynamic_slice_in_dim(table, ids[s], 1, 0) for s in range(segments)]
+        return jnp.concatenate(picked, axis=0).reshape(segments, length, rank).transpose(0, 2, 1)
+
+    positions = lax.broadcasted_iota(jnp.int32, (segments, rows // segments), 1)
+    keep = (positions < live[:, None]).reshape(rows, 1).astype(jnp.float32)
+    x_pieces, a_pieces = cols // PIECE, hidden // PIECE
+    vmem = pl.BlockSpec(memory_space=pltpu.VMEM)
+    hbm = pl.BlockSpec(memory_space=pl.ANY)
+    dma = pltpu.SemaphoreType.DMA
+    return pl.pallas_call(
+        section_kernel,
+        out_shape=jax.ShapeDtypeStruct((rows, cols), jnp.bfloat16),
+        in_specs=[vmem] * 5 + [hbm] * 2,
+        out_specs=vmem,
+        scratch_shapes=[
+            pltpu.VMEM(up_weight.shape, jnp.bfloat16),
+            pltpu.VMEM(down_weight.shape, jnp.bfloat16),
+            pltpu.VMEM((shards, x_pieces, rows, PIECE), jnp.bfloat16),
+            pltpu.VMEM((shards, a_pieces, rows, PIECE), jnp.bfloat16),
+            pltpu.VMEM((rows, cols), jnp.bfloat16),
+            pltpu.VMEM((rows, cols), jnp.float32),
+            pltpu.VMEM((shards, rank + 8, 128), jnp.float32),
+            dma((a_pieces,)), dma((shards,)),
+            dma((shards,)), dma((shards,)),
+            dma((3, shards, x_pieces)), dma((shards, x_pieces)),
+            dma((3, shards, a_pieces)), dma((shards, a_pieces)),
+            dma((2,)),
+        ],
+        compiler_params=pltpu.CompilerParams(
+            collective_id=0, has_side_effects=True, vmem_limit_bytes=VMEM_BYTES
+        ),
+    )(current, gain[None, :], keep, panels(shrink_weight, cols), panels(expand_weight, hidden),
+      up_weight, down_weight)
+
+
 def run_window(
     units, unit_ids, unit_live, gain_full, up_weight, down_weight, shrink_weight, expand_weight
 ):
@@ -117,6 +433,21 @@
     batch_list = hidden_entering.shape[0]
     row_count = hidden_entering.shape[1]
     col_count = hidden_entering.shape[2]
+    hidden = up_matrix.shape[1]
+    fits = 2 * hidden * col_count * 2 * lax.axis_size("tp") < VMEM_BYTES - 7 * 2**20
+    whole_pieces = col_count % PIECE == 0 and hidden % PIECE == 0
+    if batch_list == 1 and whole_pieces and fits and row_count <= 128:
+        produced = fused_sections(
+            hidden_entering[0],
+            segment_adapter[0],
+            segment_requests[0],
+            section_norm_gain[0],
+            up_matrix[0],
+            down_matrix[0],
+            adapter_reduce[0],
+            adapter_expand[0],
+        )
+        return produced.reshape(1, batch_list, row_count, col_count)
     collected = run_window(
         hidden_entering,
         segment_adapter,

time: 304 us -> 121 us (0.40)
  waiting for transfers between devices: 171 us -> 0 us
  Pallas kernels: 0 us -> 103 us
  matrix products: 63 us -> 0 us
  blocking collectives: 36.5 us -> 0 us
  between operations: 13.3 us -> 5.76 us
    all_gather x4 -> x0, waiting for transfers between devices: 168 us -> none  [the longest x2 125 us: block_step(): lax.all_gather(hidden_act, 'tp', axis=1, tiled=True)]
    pallas_call x0 -> x1, Pallas kernels: none -> 103 us  [fused_sections(): pl.pallas_call(section_kernel, out_shape=jax.ShapeDtypeStruct((rows, cols...]
    dot_general x8 -> x0, matrix products: 63 us -> none  [the longest x4 61.1 us: times_rows(): lax.dot_general(left, weight, (((1,), (1,)), ((), ())), preferred_element...]
    psum x2 -> x0, blocking collectives: 36.5 us -> none  [block_step(): reduced, squares = lax.psum((partial_value, local_squares), 'tp')]
    gather x2 -> x0, local copies, waits for them, and re-layouts: 8.37 us -> none  [the longest x1 4.91 us: block_step(): expand_weight[unit_ids].reshape(segments, hid_count, adapter_rank_count)]
    dynamic_slice x1 -> x2, local copies, waits for them, and re-layouts: 0.69 us -> 4.06 us  [panels(): lax.dynamic_slice_in_dim(table, ids[s], 1, 0)]
    ppermute x1 -> x0, waiting for transfers between devices: 3.36 us -> none  [shifted(): return lax.ppermute(x, axis, pairs)]
  transfers between devices with their start and end apart: 5 -> 0, of which waited for: 5 -> 0; matrix products, arithmetic and copies ran while one was open for 5% -> 0% of each run, Pallas kernels for 0% -> 0%
where the time goes in v1:
time: 121 us
  Pallas kernels  103 us (85%)
  local copies, waits for them, and re-layouts  10.3 us (9%)
  between operations  5.76 us (5%)
  other arithmetic  2.08 us (2%)
    pallas_call x1, Pallas kernels, fused_sections(): pl.pallas_call(section_kernel, out_shape=jax.ShapeDtypeStruct((rows, cols...  103 us
    dynamic_slice x2, local copies, waits for them, and re-layouts, panels(): lax.dynamic_slice_in_dim(table, ids[s], 1, 0)  4.06 us
    concatenate x12, local copies, waits for them, and re-layouts, panels(): jnp.concatenate(picked, axis=0).reshape(segments, length, rank)  2.47 us

profile of v1, /device:TPU:1, one launch (start us, length us, event | category | flops | bytes accessed | tf_op | source)
XLA Modules:
  0.0 120.8 jit_solution(16116243706179030786)
XLA Ops:
  0.0 1.4 %fusion.1 = (s32[1,1]{1,0:T(1,128)}, s32[1,1]{1,0:T(1,128)}, s32[1,1]{1,0:T(1,128)}) fusion(s32[1,3]{1,0:T(1,128)} %param.9), kind=kLoop, calls=%fused_computation.10 | loop fusion | bytes 24 | tf_op jit(solution)/shard_map/slice | solution.py:347
  7.0 2.4 %dynamic-slice_reduce_fusion.2 = (bf16[28672]{0:T(1024)(128)(2,1)S(1)}, bf16[28672]{0:T(1024)(128)(2,1)S(1)}, bf16[28672]{0:T(1024)(128)(2,1)S(1)}) fusion(bf16[1,128,28672]{2,1,0:T(8,128)(2,1)} %param.15, s32[]{:T(128)S(6)} %select_n.12, s32[]{:T(128)S(6)} %select_n.14, s32[]{:T(128)S(6)} %select_n.13), kind=kLoop, calls=%fused_computation.3 | loop fusion | bytes 344076 | tf_op jit(solution)/shard_map/dynamic_slice | solution.py:347
  9.4 0.3 concatenate.24
  9.7 0.2 copy.13
  9.9 0.3 concatenate.25
  10.3 0.2 copy.14
  10.4 0.3 concatenate.26
  10.8 0.2 copy.15
  11.0 0.7 maximum_bitcast_fusion.expand_ref
  11.7 1.7 %dynamic-slice_reduce_fusion.5 = (bf16[16384]{0:T(1024)(128)(2,1)S(1)}, bf16[16384]{0:T(1024)(128)(2,1)S(1)}, bf16[16384]{0:T(1024)(128)(2,1)S(1)}) fusion(bf16[1,128,16384]{2,1,0:T(8,128)(2,1)} %param.14, s32[]{:T(128)S(6)} %select_n.12, s32[]{:T(128)S(6)} %select_n.14, s32[]{:T(128)S(6)} %select_n.13), kind=kLoop, calls=%fused_computation.7 | loop fusion | bytes 196620 | tf_op jit(solution)/shard_map/dynamic_slice | solution.py:347
  13.4 0.2 concatenate.20
  13.6 0.1 copy.10
  13.7 0.2 concatenate.21
  13.9 0.1 copy.11
  14.0 0.2 concatenate.22
  14.2 0.1 copy.12
  14.3 0.7 maximum_bitcast_fusion.1.reduce_ref
  15.0 0.7 fusion
  15.7 0.7 reshape.60.keep_ref
  16.4 102.6 %shard_map.82 = bf16[120,1024]{1,0:T(8,128)(2,1)} custom-call(bf16[120,1024]{1,0:T(8,128)(2,1)} %bitcast.15, f32[1,8192]{1,0:T(1,128)} %gain_ref.1, f32[120,1]{1,0:T(8,128)} %reshape.60.keep_ref, bf16[3,16,1024]{2,1,0:T(8,128)(2,1)} %maximum_bitcast_fusion.1.reduce_ref, bf16[3,16,1792]{2,1,0:T(8,128)(2,1)} %maximum_bitcast_fusion.expand_ref, ...), custom_call_target="tpu_custom_call" | custom-call | tf_op jit(solution)/shard_map/pallas_call | solution.py:356
  119.1 1.7 %copy.18 = bf16[1,1,120,1024]{3,2,1,0:T(8,128)(2,1)} copy(bf16[1,1,120,1024]{3,2,1,0:T(8,128)(2,1)} %bitcast.14) | data formatting | bytes 491520

commit v2 on v1

--- a/solution.py
+++ b/solution.py
@@ -74,7 +74,7 @@
 
 
 def section_kernel(
-    x_ref, gain_ref, keep_ref, reduce_ref, expand_ref, up_hbm, down_hbm, out_ref,
+    live_ref, x_ref, gain_ref, reduce_ref, expand_ref, up_hbm, down_hbm, out_ref,
     up_v, down_v, xs, act, current, acc, partial,
     up_sem, down_sem, part_send, part_recv, x_send, x_recv, a_send, a_recv, pipe_sem,
 ):
@@ -149,38 +149,42 @@
                 send_sem=self.send.at[way, t, c], recv_sem=self.recv.at[t, c],
                 device_id={"tp": target}, device_id_type=MESH)
 
-        def each(self, source_z, c, do):
-            t = source_z * COLUMNS + x
-
-            @pl.when(jnp.logical_and(source_z <= z, z < depth - 1))
+        def each(self, source_z, column, c, do):
+            t = source_z * COLUMNS + column
+            own, first = column == x, c == 0
+            along = jnp.logical_or(own, first)
+            across = jnp.logical_and(own, jnp.logical_or(c != 0, source_z == z))
+
+            @pl.when(jnp.logical_and(along, jnp.logical_and(source_z <= z, z < depth - 1)))
             def _():
                 do(self.copy(t, c, 0, (me + COLUMNS) % shards))
 
-            @pl.when(jnp.logical_and(source_z >= z, z > 0))
+            @pl.when(jnp.logical_and(along, jnp.logical_and(source_z >= z, z > 0)))
             def _():
                 do(self.copy(t, c, 1, (me + shards - COLUMNS) % shards))
 
-            do(self.copy(t, c, 2, partner))
-
-        def forward(self, source_z, c):
-            self.each(source_z, c, lambda d: d.start())
+            @pl.when(across)
+            def _():
+                do(self.copy(t, c, 2, partner))
+
+        def forward(self, source_z, column, c):
+            self.each(source_z, column, c, lambda d: d.start())
 
         def arrive(self, t, c):
             self.copy(t, c, 2, partner).wait_recv()
 
-        def relay(self, step, c):
-            @pl.when(z >= step)
-            def _():
-                self.arrive((z - step) * COLUMNS + x, c)
-                self.forward(z - step, c)
-
-            @pl.when(z + step < depth)
-            def _():
-                self.arrive((z + step) * COLUMNS + x, c)
-                self.forward(z + step, c)
+        def pass_on(self, source_z, column, c):
+            @pl.when(jnp.logical_and(source_z >= 0, source_z < depth))
+            def _():
+                self.arrive(source_z * COLUMNS + column, c)
+                self.forward(source_z, column, c)
+
+        def relay(self, step, column, c):
+            for source_z in (z - step, z + step) if step else (z,):
+                self.pass_on(source_z, column, c)
 
         def partner_arrive(self, t):
-            @pl.loop(0, self.pieces)
+            @pl.loop(1, self.pieces)
             def _(c):
                 self.arrive(t, c)
 
@@ -189,7 +193,9 @@
             def _(source_z):
                 @pl.loop(0, self.pieces)
                 def _(c):
-                    self.each(source_z, c, lambda d: d.wait_send())
+                    self.each(source_z, x, c, lambda d: d.wait_send())
+
+                self.each(source_z, 1 - x, 0, lambda d: d.wait_send())
 
     x_side = Spread(xs, x_send, x_recv, x_pieces)
     a_side = Spread(act, a_send, a_recv, a_pieces)
@@ -198,7 +204,7 @@
         gain = gain_ref[:, pl.ds(pl.multiple_of(me * cols + c * PIECE, 128), PIECE)]
         wide = current[:, c * PIECE:(c + 1) * PIECE].astype(jnp.float32)
         xs[me, c] = (wide * gain).astype(jnp.bfloat16)
-        x_side.forward(z, c)
+        x_side.forward(z, x, c)
 
     lane_seg = lax.broadcasted_iota(jnp.int32, (1, 128), 1) // seg_rows
     nt = (((1,), (1,)), ((), ()))
@@ -231,10 +237,13 @@
     def _(i):
         part_copy(me, (me + i) % shards).start()
 
+    x_side.relay(0, 1 - x, 0)
     for step in range(1, depth):
         @pl.loop(0, x_pieces)
         def _(c):
-            x_side.relay(step, c)
+            x_side.relay(step, x, c)
+
+        x_side.relay(step, 1 - x, 0)
 
     @pl.loop(1, shards)
     def _(i):
@@ -257,7 +266,7 @@
     def _(source_z):
         x_side.partner_arrive(source_z * COLUMNS + (1 - x))
 
-    LAG = 2
+    LAG = 3
 
     def relays(k):
         for step in range(1, depth):
@@ -265,7 +274,12 @@
 
             @pl.when(jnp.logical_and(c >= 0, c < a_pieces))
             def _():
-                a_side.relay(step, c)
+                a_side.relay(step, x, c)
+
+        for step in range(depth):
+            @pl.when(k == LAG * (step + 1))
+            def _():
+                a_side.relay(step, 1 - x, 0)
 
     @pl.loop(0, a_pieces)
     def _(k):
@@ -280,7 +294,7 @@
         adapted = jnp.dot(low_rank, panel, preferred_element_type=jnp.float32)
         value = inverse * base + adapted
         act[me, k] = (value / (1.0 + jnp.exp(-value))).astype(jnp.bfloat16)
-        a_side.forward(z, k)
+        a_side.forward(z, x, k)
         relays(k)
 
     acc[...] = current[...].astype(jnp.float32)
@@ -308,19 +322,23 @@
 
             down_part(t)
 
-    order = [(0, 0), (0, 1), (1, 0), (-1, 0), (2, 0), (-2, 0)]
+    order = [[(0, 0)], [(0, 1)], [(1, 0)], [(-1, 0)], [(1, 1), (-1, 1)], [(2, 0), (-2, 0)], [(2, 1), (-2, 1)], [], []]
+    begun = [item for items in order for item in items]
     rest = [(d * sign, o) for d in range(1, depth) for o in (0, 1) for sign in (1, -1)]
-    rest = [item for item in rest if item not in order]
     ticks = LAG * (depth - 1)
-    for j in range(ticks):
-        relays(a_pieces + j)
-        if j < len(order):
-            far, other = order[j]
+    order += [[item for item in rest if item not in begun]]
+    for j in range(max(ticks, len(order))):
+        if j < ticks:
+            relays(a_pieces + j)
+        for far, other in order[j] if j < len(order) else ():
             down_at(z + far, (x + other) % COLUMNS)
-    for far, other in order[ticks:] + rest:
-        down_at(z + far, (x + other) % COLUMNS)
-
-    out_ref[...] = jnp.where(keep_ref[...] > 0.0, acc[...], 0.0).astype(jnp.bfloat16)
+
+    row = lax.broadcasted_iota(jnp.int32, (rows, 1), 0)
+    kept = row < 0
+    for s in range(segments):
+        low = s * seg_rows
+        kept = jnp.logical_or(kept, jnp.logical_and(row >= low, row < low + jnp.minimum(live_ref[s], seg_rows)))
+    out_ref[...] = jnp.where(kept, acc[...], 0.0).astype(jnp.bfloat16)
 
     @pl.when(stage < stages - 1)
     def _():
@@ -347,8 +365,6 @@
         picked = [lax.dynamic_slice_in_dim(table, ids[s], 1, 0) for s in range(segments)]
         return jnp.concatenate(picked, axis=0).reshape(segments, length, rank).transpose(0, 2, 1)
 
-    positions = lax.broadcasted_iota(jnp.int32, (segments, rows // segments), 1)
-    keep = (positions < live[:, None]).reshape(rows, 1).astype(jnp.float32)
     x_pieces, a_pieces = cols // PIECE, hidden // PIECE
     vmem = pl.BlockSpec(memory_space=pltpu.VMEM)
     hbm = pl.BlockSpec(memory_space=pl.ANY)
@@ -356,7 +372,7 @@
     return pl.pallas_call(
         section_kernel,
         out_shape=jax.ShapeDtypeStruct((rows, cols), jnp.bfloat16),
-        in_specs=[vmem] * 5 + [hbm] * 2,
+        in_specs=[pl.BlockSpec(memory_space=pltpu.SMEM)] + [vmem] * 4 + [hbm] * 2,
         out_specs=vmem,
         scratch_shapes=[
             pltpu.VMEM(up_weight.shape, jnp.bfloat16),
@@ -375,7 +391,7 @@
         compiler_params=pltpu.CompilerParams(
             collective_id=0, has_side_effects=True, vmem_limit_bytes=VMEM_BYTES
         ),
-    )(current, gain[None, :], keep, panels(shrink_weight, cols), panels(expand_weight, hidden),
+    )(live, current, gain[None, :], panels(shrink_weight, cols), panels(expand_weight, hidden),
       up_weight, down_weight)
 
 
@@ -435,7 +451,7 @@
     col_count = hidden_entering.shape[2]
     hidden = up_matrix.shape[1]
     fits = 2 * hidden * col_count * 2 * lax.axis_size("tp") < VMEM_BYTES - 7 * 2**20
-    whole_pieces = col_count % PIECE == 0 and hidden % PIECE == 0
+    whole_pieces = col_count % PIECE == 0 and hidden % PIECE == 0 and hidden >= 4 * PIECE
     if batch_list == 1 and whole_pieces and fits and row_count <= 128:
         produced = fused_sections(
             hidden_entering[0],

time: 121 us -> 121 us (level)
  no operation moved by 1% of the time
where the time goes in v2:
time: 121 us
  Pallas kernels  104 us (86%)
  local copies, waits for them, and re-layouts  9.57 us (8%)
  between operations  5.76 us (5%)
  other arithmetic  1.36 us (1%)
    pallas_call x1, Pallas kernels, fused_sections(): pl.pallas_call(section_kernel, out_shape=jax.ShapeDtypeStruct((rows, cols...  104 us
    dynamic_slice x2, local copies, waits for them, and re-layouts, panels(): lax.dynamic_slice_in_dim(table, ids[s], 1, 0)  4.09 us
    concatenate x12, local copies, waits for them, and re-layouts, panels(): jnp.concatenate(picked, axis=0).reshape(segments, length, rank)  2.47 us

profile of v2, /device:TPU:1, one launch (start us, length us, event | category | flops | bytes accessed | tf_op | source)
XLA Modules:
  0.0 120.5 jit_solution(7777597147645322204)
XLA Ops:
  0.0 1.4 %fusion = (s32[1,1]{1,0:T(1,128)}, s32[1,1]{1,0:T(1,128)}, s32[1,1]{1,0:T(1,128)}) fusion(s32[1,3]{1,0:T(1,128)} %param.9), kind=kLoop, calls=%fused_computation.8 | loop fusion | bytes 24 | tf_op jit(solution)/shard_map/slice | solution.py:365
  7.0 2.4 %dynamic-slice_reduce_fusion.2 = (bf16[28672]{0:T(1024)(128)(2,1)S(1)}, bf16[28672]{0:T(1024)(128)(2,1)S(1)}, bf16[28672]{0:T(1024)(128)(2,1)S(1)}) fusion(bf16[1,128,28672]{2,1,0:T(8,128)(2,1)} %param.15, s32[]{:T(128)S(6)} %select_n.12, s32[]{:T(128)S(6)} %select_n.14, s32[]{:T(128)S(6)} %select_n.13), kind=kLoop, calls=%fused_computation.3 | loop fusion | bytes 344076 | tf_op jit(solution)/shard_map/dynamic_slice | solution.py:365
  9.4 0.3 concatenate.24
  9.8 0.2 copy.12
  9.9 0.3 concatenate.25
  10.3 0.2 copy.13
  10.5 0.3 concatenate.26
  10.8 0.2 copy.14
  11.0 0.7 maximum_bitcast_fusion.expand_ref
  11.7 1.7 %dynamic-slice_reduce_fusion.5 = (bf16[16384]{0:T(1024)(128)(2,1)S(1)}, bf16[16384]{0:T(1024)(128)(2,1)S(1)}, bf16[16384]{0:T(1024)(128)(2,1)S(1)}) fusion(bf16[1,128,16384]{2,1,0:T(8,128)(2,1)} %param.14, s32[]{:T(128)S(6)} %select_n.12, s32[]{:T(128)S(6)} %select_n.14, s32[]{:T(128)S(6)} %select_n.13), kind=kLoop, calls=%fused_computation.7 | loop fusion | bytes 196620 | tf_op jit(solution)/shard_map/dynamic_slice | solution.py:365
  13.4 0.2 concatenate.21
  13.6 0.1 copy.10
  13.7 0.2 concatenate.22
  13.9 0.1 copy.11
  14.0 0.2 concatenate.20
  14.3 0.1 copy.9
  14.4 0.7 maximum_bitcast_fusion.1.reduce_ref
  15.0 103.8 %shard_map.82 = bf16[120,1024]{1,0:T(8,128)(2,1)} custom-call(s32[3]{0:T(128)} %bitcast.16, bf16[120,1024]{1,0:T(8,128)(2,1)} %bitcast.15, f32[1,8192]{1,0:T(1,128)} %gain_ref.1, bf16[3,16,1024]{2,1,0:T(8,128)(2,1)} %maximum_bitcast_fusion.1.reduce_ref, bf16[3,16,1792]{2,1,0:T(8,128)(2,1)} %maximum_bitcast_fusion.expand_ref, bf16[1792,8192]{1,0:T(8,128)(2,1)} %bitcast.12, ...), custom_call_target="tpu_custom_call" | custom-call | tf_op jit(solution)/shard_map/pallas_call | solution.py:372
  118.9 1.7 %copy.16 = bf16[1,1,120,1024]{3,2,1,0:T(8,128)(2,1)} copy(bf16[1,1,120,1024]{3,2,1,0:T(8,128)(2,1)} %bitcast.14) | data formatting | bytes 491520
